TPU v7x, 32 devices: a whole 2x2x4 slice. The times are simulated.
32 devices in a mesh: samp: 8 (over z, core), var: 4 (over y, x).
Axes of the slice: x: 2, y: 2, z: 4, core: 2. Of those that a mesh axis runs over, the one named last changes fastest.
Arguments:
- hap_words: int32 [2, 512, 512], P(None, 'samp', 'var'), may hold values from 0 to 1073741823
- total_counts: int32 [15360, 8192], P('samp', 'var'), may hold values from 0 to 4999
- allele_one: int32 [15360, 8192], P('samp', 'var'), may hold values from 0 to 299
- allele_two: int32 [15360, 8192], P('samp', 'var'), may hold values from 0 to 299
Outputs:
- z_total: float32 [512, 8192], P('samp', 'var')
- z_allelic: float32 [512, 8192], P('samp', 'var')
Inputs may be any that keep to these rules, and one draw needn't show every extreme that they name: Bit k, for k below 30, of hap_words[c, j, v] is haplotype c of sample 30 * j + k at variant v; higher bits are zero.
All inputs are finite; a program needn't handle non-finite values.
Results may differ from a plain program's by a relative error of at most 0.0003.
The roundings to bfloat16 on the way count: a program that leaves them out, or rounds other values in their place, can miss the bound.
Values sent between devices are 32-bit elements; how exact they have to be, the bound alone decides.
A program may use at most 192 MiB of HBM per device.

v0:
```python
import jax
import jax.numpy as jnp
from jax import lax
from jax.sharding import PartitionSpec as P

BITS = 30


def unpack(packed):
    shifts = jnp.arange(BITS, dtype=jnp.int32)
    bit_table = jnp.bitwise_and(
        jnp.right_shift(packed[:, :, None, :], shifts[None, None, :, None]), 1
    )
    return bit_table.reshape(2, packed.shape[1] * BITS, packed.shape[2])


def features(total_part, one_part, two_part):
    log_total = jnp.log1p(total_part.astype(jnp.float32))
    one_plus = one_part.astype(jnp.float32) + 1.0
    two_plus = two_part.astype(jnp.float32) + 1.0
    log_ratio = jnp.log(one_plus / two_plus)
    weight = 1.0 / (1.0 / one_plus + 1.0 / two_plus)
    return (log_total, (weight * log_ratio).astype(jnp.bfloat16), weight.astype(jnp.bfloat16))


def finish(pair_sums, dos_margin, gene_margin, sample_count):
    dos_sum, dos_sq = (dos_margin[0], dos_margin[1])
    gene_sum, gene_sq = (gene_margin[0], gene_margin[1])
    dosage_var = dos_sq - dos_sum * dos_sum / sample_count
    gene_var = gene_sq - gene_sum * gene_sum / sample_count
    covariance = pair_sums[0] - dos_sum[:, None] * gene_sum[None, :] / sample_count
    z_total = (
        jnp.sqrt(sample_count)
        * covariance
        / jnp.sqrt((dosage_var[:, None] + 1.0) * (gene_var[None, :] + 1.0))
    )
    z_allelic = pair_sums[1] / jnp.sqrt(pair_sums[2] + 1.0)
    return (z_total, z_allelic)


def per_device(hap_words, total_counts, allele_one, allele_two):
    panel_words = lax.all_gather(hap_words, "var", axis=2, tiled=True)
    bit_table = unpack(panel_words)
    dosage_b = (bit_table[0] + bit_table[1] - 1).astype(jnp.bfloat16)
    phase_int = bit_table[0] - bit_table[1]
    phase_b = phase_int.astype(jnp.bfloat16)
    phase_sq_b = (phase_int * phase_int).astype(jnp.bfloat16)
    dos_margin = jnp.stack(
        [
            jnp.sum(dosage_b, axis=0, dtype=jnp.float32),
            jnp.sum(dosage_b * dosage_b, axis=0, dtype=jnp.float32),
        ]
    )
    log_total, weighted_b, weight_b = features(total_counts, allele_one, allele_two)
    gene_margin = jnp.stack([jnp.sum(log_total, axis=0), jnp.sum(log_total * log_total, axis=0)])
    cross_total = jnp.einsum(
        "sv,sg->vg", dosage_b, log_total.astype(jnp.bfloat16), preferred_element_type=jnp.float32
    )
    cross_allelic = jnp.einsum("sv,sg->vg", phase_b, weighted_b, preferred_element_type=jnp.float32)
    het_weight = jnp.einsum("sv,sg->vg", phase_sq_b, weight_b, preferred_element_type=jnp.float32)
    pair_sums = jnp.stack([cross_total, cross_allelic, het_weight])
    sample_groups = lax.axis_size("samp")
    sample_count = jnp.float32(bit_table.shape[1] * sample_groups)
    own_pairs, own_dos = (
        lax.psum_scatter(pair_sums, "samp", scatter_dimension=1, tiled=True),
        lax.psum_scatter(dos_margin, "samp", scatter_dimension=1, tiled=True),
    )
    summed_genes = lax.psum(gene_margin, "samp")
    return finish(own_pairs, own_dos, summed_genes, sample_count)


def solution(mesh):
    in_specs = (P(None, "samp", "var"), P("samp", "var"), P("samp", "var"), P("samp", "var"))
    out_specs = (P("samp", "var"), P("samp", "var"))
    return jax.shard_map(
        per_device, mesh=mesh, in_specs=in_specs, out_specs=out_specs, check_vma=False
    )
```

profile of v0, /device:TPU:0, one launch (start us, length us, event | category | flops | bytes accessed | tf_op | source)
XLA Modules:
  0.0 234.2 jit_solution(2295800869853956210)
XLA Ops:
  7.2 0.0 reduce-scatter.7.cloned.1.call-start
  7.2 11.8 %all_gather.3 = s32[2,64,512]{2,1,0:T(8,128)S(1)} all-gather(s32[2,64,128]{2,1,0:T(8,128)} %param.4), channel_id=1, replica_groups=mesh['samp'=8,'var'=4] {'var'}, dimensions={2}, use_global_device_ids=true | all-gather | bytes 327680 | tf_op jit(solution)/shard_map/all_gather | solution.py:42
  19.0 1.3 shift-right-arithmetic_and_fusion
  20.3 0.0 copy-start
  20.3 3.2 %copy-done = s32[2,64,30,512]{3,2,1,0:T(8,128)} copy-done((s32[2,64,30,512]{3,2,1,0:T(8,128)}, s32[2,64,30,512]{3,2,1,0:T(8,128)S(1)}, u32[]{:S(2)}) %copy-start) | copy-done | bytes 7864344
  23.5 1.4 convert_reduce_fusion.1
  24.9 0.9 copy.6
  25.8 0.0 reduce-scatter.7.cloned.1.call-update
  25.8 0.2 reduce-scatter.5.cloned.1.call-start
  26.0 6.9 %fusion.14 = (bf16[1,64,30,512]{3,2,1,0:T(8,128)(2,1)}, bf16[1,64,30,512]{3,2,1,0:T(8,128)(2,1)}) fusion(s32[2,64,30,512]{3,2,1,0:T(8,128)} %copy-done), kind=kLoop, calls=%fused_computation.22 | loop fusion | flops 3932160 | bytes 11796480 | tf_op jit(solution)/shard_map/convert_element_type | solution.py:46
  32.9 1.5 convert_element_type.47
  34.4 2.6 %convert_element_type.51 = bf16[1920,512]{1,0:T(8,128)(2,1)S(1)} reshape(bf16[1,64,30,512]{3,2,1,0:T(8,128)(2,1)} %get-tuple-element.7) | data formatting | bytes 3932160 | tf_op jit(solution)/shard_map/convert_element_type | solution.py:46
  37.0 3.9 %convert_element_type.56 = bf16[1920,512]{1,0:T(8,128)(2,1)} reshape(bf16[1,64,30,512]{3,2,1,0:T(8,128)(2,1)} %get-tuple-element.8) | data formatting | bytes 3932160 | tf_op jit(solution)/shard_map/convert_element_type | solution.py:47
  40.9 0.0 copy-start.2
  40.9 14.6 %fusion.7 = f32[1,512,2048]{2,1,0:T(8,128)S(1)} fusion(bf16[1920,512]{1,0:T(8,128)(2,1)S(1)} %convert_element_type.51, s32[1920,2048]{1,0:T(8,128)} %param.6, s32[1920,2048]{1,0:T(8,128)} %param.7), kind=kOutput, calls=%fused_computation.19 | convolution fusion | flops 4069785600 | bytes 37617664 | tf_op jit(solution)/shard_map/sv,sg->vg/dot_general | solution.py:59
  55.5 0.0 copy-done.2
  55.5 0.0 copy-start.1
  55.5 15.1 %fusion.8 = f32[1,512,2048]{2,1,0:T(8,128)} fusion(bf16[1920,512]{1,0:T(8,128)(2,1)S(1)} %copy-done.2, s32[1920,2048]{1,0:T(8,128)} %param.6, s32[1920,2048]{1,0:T(8,128)} %param.7), kind=kOutput, calls=%fused_computation.20 | convolution fusion | flops 4061921280 | bytes 37617664 | tf_op jit(solution)/shard_map/sv,sg->vg/dot_general | solution.py:60
  70.7 0.0 copy-done.1
  70.7 12.8 %fusion.11 = f32[1,512,2048]{2,1,0:T(8,128)} fusion(bf16[1920,512]{1,0:T(8,128)(2,1)S(1)} %copy-done.1, s32[1920,2048]{1,0:T(8,128)} %param.5), kind=kOutput, calls=%fused_computation.21 | convolution fusion | flops 4034396160 | bytes 21889024 | tf_op jit(solution)/shard_map/sv,sg->vg/dot_general | solution.py:56
  83.5 9.9 %pad_maximum_fusion = f32[3,512,2048]{2,1,0:T(8,128)} fusion(f32[1,512,2048]{2,1,0:T(8,128)} %fusion.8, f32[1,512,2048]{2,1,0:T(8,128)S(1)} %fusion.7, f32[1,512,2048]{2,1,0:T(8,128)} %fusion.11), kind=kLoop, calls=%fused_computation.8 | loop fusion | flops 6291456 | bytes 25165824 | tf_op jit(solution)/shard_map/stack | solution.py:61
  93.4 0.0 reduce-scatter.5.cloned.1.call-update
  93.4 12.1 %fusion = (f32[2048]{0:T(1024)S(1)}, f32[2048]{0:T(1024)S(1)}) fusion(s32[1920,2048]{1,0:T(8,128)} %param.5), kind=kLoop, calls=%fused_computation.6 | loop fusion | flops 15724544 | bytes 15745024 | tf_op jit(solution)/shard_map/reduce_sum | solution.py:55
  105.5 28.7 %psum.7 = f32[2,2048]{1,0:T(2,128)S(1)} all-reduce(f32[2,2048]{1,0:T(2,128)S(1)} %pad_maximum_fusion.1), channel_id=1, replica_groups=mesh['samp'=8,'var'=4] {'samp'}, use_global_device_ids=true, to_apply=%region_6.0 | all-reduce | flops 4096 | bytes 32768 | tf_op jit(solution)/shard_map/psum | solution.py:68
  134.2 0.0 reduce-scatter.7.cloned.1.call-done
  134.2 0.9 fusion.24
  135.2 0.1 copy.8
  135.2 0.1 copy.9
  135.3 87.9 %reduce-scatter.5.cloned.1.call-done = f32[3,64,2048]{2,1,0:T(8,128)} async-done(((f32[3,512,2048]{2,1,0:T(8,128)}), f32[3,64,2048]{2,1,0:T(8,128)}) %reduce-scatter.5.cloned.1.call-update) | async-done | bytes 1572880 | tf_op jit(solution)/shard_map/reduce_scatter | solution.py:65
  223.2 2.1 fusion.17
  225.3 2.0 fusion.20
  (4 shorter events, 0.1 us)
Async XLA Ops:
  7.2 127.1 %reduce-scatter.7.cloned.1.call-start = ((), (), s32[]{:S(2)}) async-start(), calls=%async_computation.3 | async-start | bytes 294912
  20.3 3.2 %copy-start = (s32[2,64,30,512]{3,2,1,0:T(8,128)}, s32[2,64,30,512]{3,2,1,0:T(8,128)S(1)}, u32[]{:S(2)}) copy-start(s32[2,64,30,512]{3,2,1,0:T(8,128)S(1)} %shift-right-arithmetic_and_fusion) | copy-start | bytes 23592964
  25.8 197.5 %reduce-scatter.5.cloned.1.call-start = ((), (), s32[]{:S(2)}) async-start(), calls=%async_computation.2 | async-start | bytes 14155776 | tf_op jit(solution)/shard_map/reduce_scatter | solution.py:65
  40.9 14.6 %copy-start.2 = (bf16[1920,512]{1,0:T(8,128)(2,1)S(1)}, bf16[1920,512]{1,0:T(8,128)(2,1)}, u32[]{:S(2)}) copy-start(bf16[1920,512]{1,0:T(8,128)(2,1)} %convert_element_type.56) | copy-start | bytes 5898244
  55.5 15.2 %copy-start.1 = (bf16[1920,512]{1,0:T(8,128)(2,1)S(1)}, bf16[1920,512]{1,0:T(8,128)(2,1)}, u32[]{:S(2)}) copy-start(bf16[1920,512]{1,0:T(8,128)(2,1)} %convert_element_type.47) | copy-start | bytes 5898244
Sparse Core Ops, SparseCore 0:
  25.9 30.7 reduce-scatter.6
  93.5 129.7 reduce-scatter.4
where the time goes:
time: 235 us; the launch traced here: 234 us
  waiting for transfers between devices  88 us (37%)
  matrix products  42.6 us (18%)
  blocking collectives  40.5 us (17%)
  other arithmetic  35.6 us (15%)
  between operations  14.1 us (6%)
  local copies, waits for them, and re-layouts  13.1 us (6%)
    reduce_scatter x1, waiting for transfers between devices, per_device(): lax.psum_scatter(pair_sums, 'samp', scatter_dimension=1, tiled=True)  87.9 us
    psum x1, blocking collectives, per_device(): summed_genes = lax.psum(gene_margin, 'samp')  28.7 us
    dot_general x1, matrix products, per_device(): jnp.einsum('sv,sg->vg', phase_sq_b, weight_b, preferred_element_type=jnp....  15.1 us
    dot_general x1, matrix products, per_device(): jnp.einsum('sv,sg->vg', phase_b, weighted_b, preferred_element_type=jnp.f...  14.6 us
    dot_general x1, matrix products, per_device(): jnp.einsum('sv,sg->vg', dosage_b, log_total.astype(jnp.bfloat16), preferr...  12.8 us
    reduce_sum x1, other arithmetic, per_device(): jnp.sum(log_total, axis=0)  12.1 us
    all_gather x1, blocking collectives, per_device(): panel_words = lax.all_gather(hap_words, 'var', axis=2, tiled=True)  11.8 us
    another operation x1, other arithmetic, per_device(): pair_sums = jnp.stack([cross_total, cross_allelic, het_weight])  9.86 us
  transfers between devices with their start and end apart: 2, of which 1 were waited for; matrix products, arithmetic and copies ran while one was open for 34% of the time, Pallas kernels for 0%

commit v1 on v0

--- a/solution.py
+++ b/solution.py
@@ -65,7 +65,11 @@
         lax.psum_scatter(pair_sums, "samp", scatter_dimension=1, tiled=True),
         lax.psum_scatter(dos_margin, "samp", scatter_dimension=1, tiled=True),
     )
-    summed_genes = lax.psum(gene_margin, "samp")
+    summed_genes = gene_margin
+    for hop in (1, 2, 4):
+        summed_genes = summed_genes + lax.ppermute(
+            summed_genes, "samp", [(dev, dev ^ hop) for dev in range(8)]
+        )
     return finish(own_pairs, own_dos, summed_genes, sample_count)
 
 

time: 235 us -> 241 us (1.026)
  blocking collectives: 40.5 us -> 11.8 us
  waiting for transfers between devices: 88 us -> 112 us
  matrix products: 42.6 us -> 47.5 us
  starting transfers between devices: 0.26 us -> 4.57 us
    psum x1 -> x0, blocking collectives: 28.7 us -> none  [per_device(): summed_genes = lax.psum(gene_margin, 'samp')]
    reduce_scatter x1, waiting for transfers between devices: 87.9 us -> 107 us  [per_device(): lax.psum_scatter(pair_sums, 'samp', scatter_dimension=1, tiled=True)]
    ppermute x0 -> x3, waiting for transfers between devices: none -> 5.57 us  [per_device(): lax.ppermute(summed_genes, 'samp', [(dev, dev ^ hop) for dev in range(8)])]
    ppermute x0 -> x3, starting transfers between devices: none -> 4.31 us  [per_device(): lax.ppermute(summed_genes, 'samp', [(dev, dev ^ hop) for dev in range(8)])]
    dot_general x1, matrix products: 12.8 us -> 15.3 us  [per_device(): jnp.einsum('sv,sg->vg', dosage_b, log_total.astype(jnp.bfloat16), preferr...]
  transfers between devices with their start and end apart: 2 -> 5, of which waited for: 1 -> 4; matrix products, arithmetic and copies ran while one was open for 34% -> 36% of each run, Pallas kernels for 0% -> 0%
where the time goes in v1:
time: 241 us; the launch traced here: 240 us
  waiting for transfers between devices  112 us (46%)
  matrix products  47.5 us (20%)
  other arithmetic  35.8 us (15%)
  local copies, waits for them, and re-layouts  14.4 us (6%)
  between operations  14.1 us (6%)
  blocking collectives  11.8 us (5%)
  starting transfers between devices  4.57 us (2%)
    reduce_scatter x1, waiting for transfers between devices, per_device(): lax.psum_scatter(pair_sums, 'samp', scatter_dimension=1, tiled=True)  107 us
    dot_general x1, matrix products, per_device(): jnp.einsum('sv,sg->vg', phase_b, weighted_b, preferred_element_type=jnp.f...  16.4 us
    dot_general x1, matrix products, per_device(): jnp.einsum('sv,sg->vg', phase_sq_b, weight_b, preferred_element_type=jnp....  15.8 us
    dot_general x1, matrix products, per_device(): jnp.einsum('sv,sg->vg', dosage_b, log_total.astype(jnp.bfloat16), preferr...  15.3 us
    reduce_sum x1, other arithmetic, per_device(): jnp.sum(log_total, axis=0)  12.3 us
    all_gather x1, blocking collectives, per_device(): panel_words = lax.all_gather(hap_words, 'var', axis=2, tiled=True)  11.8 us
    another operation x1, other arithmetic, per_device(): pair_sums = jnp.stack([cross_total, cross_allelic, het_weight])  9.86 us
    convert_element_type x1, other arithmetic, per_device(): phase_b = phase_int.astype(jnp.bfloat16)  6.77 us
  transfers between devices with their start and end apart: 5, of which 4 were waited for; matrix products, arithmetic and copies ran while one was open for 36% of the time, Pallas kernels for 0%

profile of v1, /device:TPU:0, one launch (start us, length us, event | category | flops | bytes accessed | tf_op | source)
XLA Modules:
  0.0 240.4 jit_solution(15230521868294346213)
XLA Ops:
  7.2 0.0 reduce-scatter.7.cloned.1.call-start
  7.2 11.8 %all_gather.3 = s32[2,64,512]{2,1,0:T(8,128)S(1)} all-gather(s32[2,64,128]{2,1,0:T(8,128)} %param.4), channel_id=1, replica_groups=mesh['samp'=8,'var'=4] {'var'}, dimensions={2}, use_global_device_ids=true | all-gather | bytes 327680 | tf_op jit(solution)/shard_map/all_gather | solution.py:42
  19.0 1.3 shift-right-arithmetic_and_fusion
  20.3 0.0 copy-start
  20.3 3.2 %copy-done = s32[2,64,30,512]{3,2,1,0:T(8,128)} copy-done((s32[2,64,30,512]{3,2,1,0:T(8,128)}, s32[2,64,30,512]{3,2,1,0:T(8,128)S(1)}, u32[]{:S(2)}) %copy-start) | copy-done | bytes 7864344
  23.5 1.4 convert_reduce_fusion.1
  24.9 0.9 copy.6
  25.8 0.0 reduce-scatter.7.cloned.1.call-update
  25.8 0.2 reduce-scatter.5.cloned.1.call-start
  26.0 6.8 %fusion.14 = (bf16[1,64,30,512]{3,2,1,0:T(8,128)(2,1)}, bf16[1,64,30,512]{3,2,1,0:T(8,128)(2,1)}) fusion(s32[2,64,30,512]{3,2,1,0:T(8,128)} %copy-done), kind=kLoop, calls=%fused_computation.22 | loop fusion | flops 3932160 | bytes 11796480 | tf_op jit(solution)/shard_map/convert_element_type | solution.py:46
  32.8 3.9 %convert_element_type.56 = bf16[1920,512]{1,0:T(8,128)(2,1)} reshape(bf16[1,64,30,512]{3,2,1,0:T(8,128)(2,1)} %get-tuple-element.8) | data formatting | bytes 3932160 | tf_op jit(solution)/shard_map/convert_element_type | solution.py:47
  36.7 3.8 %convert_element_type.51 = bf16[1920,512]{1,0:T(8,128)(2,1)} reshape(bf16[1,64,30,512]{3,2,1,0:T(8,128)(2,1)} %get-tuple-element.7) | data formatting | bytes 3932160 | tf_op jit(solution)/shard_map/convert_element_type | solution.py:46
  40.5 0.0 copy-start.2
  40.5 15.8 %fusion.8 = f32[1,512,2048]{2,1,0:T(8,128)} fusion(bf16[1920,512]{1,0:T(8,128)(2,1)} %convert_element_type.56, s32[1920,2048]{1,0:T(8,128)} %param.6, s32[1920,2048]{1,0:T(8,128)} %param.7), kind=kOutput, calls=%fused_computation.20 | convolution fusion | flops 4061921280 | bytes 37617664 | tf_op jit(solution)/shard_map/sv,sg->vg/dot_general | solution.py:60
  56.3 0.0 copy-done.2
  56.3 16.4 %fusion.7 = f32[1,512,2048]{2,1,0:T(8,128)} fusion(bf16[1920,512]{1,0:T(8,128)(2,1)S(1)} %copy-done.2, s32[1920,2048]{1,0:T(8,128)} %param.6, s32[1920,2048]{1,0:T(8,128)} %param.7), kind=kOutput, calls=%fused_computation.19 | convolution fusion | flops 4069785600 | bytes 37617664 | tf_op jit(solution)/shard_map/sv,sg->vg/dot_general | solution.py:59
  72.7 1.6 convert_element_type.47
  74.3 0.0 copy-start.1
  74.3 15.3 %fusion.11 = f32[1,512,2048]{2,1,0:T(8,128)} fusion(bf16[1920,512]{1,0:T(8,128)(2,1)} %convert_element_type.47, s32[1920,2048]{1,0:T(8,128)} %param.5), kind=kOutput, calls=%fused_computation.21 | convolution fusion | flops 4034396160 | bytes 21889024 | tf_op jit(solution)/shard_map/sv,sg->vg/dot_general | solution.py:56
  89.6 0.0 copy-done.1
  89.6 9.9 %pad_maximum_fusion = f32[3,512,2048]{2,1,0:T(8,128)} fusion(f32[1,512,2048]{2,1,0:T(8,128)S(1)} %copy-done.1, f32[1,512,2048]{2,1,0:T(8,128)} %fusion.7, f32[1,512,2048]{2,1,0:T(8,128)} %fusion.11), kind=kLoop, calls=%fused_computation.8 | loop fusion | flops 6291456 | bytes 25165824 | tf_op jit(solution)/shard_map/stack | solution.py:61
  99.5 0.0 reduce-scatter.5.cloned.1.call-update
  99.5 12.3 %fusion = (f32[2048]{0:T(1024)S(1)}, f32[2048]{0:T(1024)S(1)}) fusion(s32[1920,2048]{1,0:T(8,128)} %param.5), kind=kLoop, calls=%fused_computation.6 | loop fusion | flops 15724544 | bytes 15745024 | tf_op jit(solution)/shard_map/reduce_sum | solution.py:55
  111.9 0.1 collective-permute-start
  111.9 1.2 collective-permute-done
  113.1 1.6 collective-permute-start.1
  114.8 0.0 reduce-scatter.7.cloned.1.call-done
  114.8 0.9 fusion.25
  115.7 0.1 copy.9
  115.8 0.1 copy.8
  115.8 1.7 collective-permute-done.1
  117.5 2.6 %collective-permute-start.2 = (f32[2,2048]{1,0:T(2,128)S(1)}, f32[2,2048]{1,0:T(2,128)S(1)}, u32[]{:S(2)}, u32[]{:S(2)}) collective-permute-start(f32[2,2048]{1,0:T(2,128)S(1)} %fusion.30), channel_id=1, source_target_pairs={{0,16},{4,20},{8,24},{12,28},{16,0},{20,4},{24,8},{28,12},{1,17},{... | collective-permute-start | bytes 49160 | tf_op jit(solution)/shard_map/ppermute | solution.py:70
  120.1 2.7 %collective-permute-done.2 = f32[2,2048]{1,0:T(2,128)S(1)} collective-permute-done((f32[2,2048]{1,0:T(2,128)S(1)}, f32[2,2048]{1,0:T(2,128)S(1)}, u32[]{:S(2)}, u32[]{:S(2)}) %collective-permute-start.2) | collective-permute-done | bytes 16416 | tf_op jit(solution)/shard_map/ppermute | solution.py:70
  122.9 106.6 %reduce-scatter.5.cloned.1.call-done = f32[3,64,2048]{2,1,0:T(8,128)} async-done(((f32[3,512,2048]{2,1,0:T(8,128)}), f32[3,64,2048]{2,1,0:T(8,128)}) %reduce-scatter.5.cloned.1.call-update) | async-done | bytes 1572880 | tf_op jit(solution)/shard_map/reduce_scatter | solution.py:65
  229.5 2.1 fusion.17
  231.5 2.0 fusion.20
  (7 shorter events, 0.1 us)
Async XLA Ops:
  7.2 107.6 %reduce-scatter.7.cloned.1.call-start = ((), (), s32[]{:S(2)}) async-start(), calls=%async_computation.3 | async-start | bytes 294912
  20.3 3.2 %copy-start = (s32[2,64,30,512]{3,2,1,0:T(8,128)}, s32[2,64,30,512]{3,2,1,0:T(8,128)S(1)}, u32[]{:S(2)}) copy-start(s32[2,64,30,512]{3,2,1,0:T(8,128)S(1)} %shift-right-arithmetic_and_fusion) | copy-start | bytes 23592964
  25.8 203.7 %reduce-scatter.5.cloned.1.call-start = ((), (), s32[]{:S(2)}) async-start(), calls=%async_computation.2 | async-start | bytes 14155776 | tf_op jit(solution)/shard_map/reduce_scatter | solution.py:65
  40.5 15.8 %copy-start.2 = (bf16[1920,512]{1,0:T(8,128)(2,1)S(1)}, bf16[1920,512]{1,0:T(8,128)(2,1)}, u32[]{:S(2)}) copy-start(bf16[1920,512]{1,0:T(8,128)(2,1)} %convert_element_type.51) | copy-start | bytes 5898244
  74.3 15.3 %copy-start.1 = (f32[1,512,2048]{2,1,0:T(8,128)S(1)}, f32[1,512,2048]{2,1,0:T(8,128)}, u32[]{:S(2)}) copy-start(f32[1,512,2048]{2,1,0:T(8,128)} %fusion.8) | copy-start | bytes 12582916
  111.9 1.2 collective-permute-start
  113.1 4.3 %collective-permute-start.1 = (f32[2,2048]{1,0:T(2,128)S(1)}, f32[2,2048]{1,0:T(2,128)S(1)}, u32[]{:S(2)}, u32[]{:S(2)}) collective-permute-start(f32[2,2048]{1,0:T(2,128)S(1)} %fusion.24), channel_id=1, source_target_pairs={{0,8},{4,12},{8,0},{12,4},{16,24},{20,28},{24,16},{28,20},{1,9},{5... | collective-permute-start | bytes 49160 | tf_op jit(solution)/shard_map/ppermute | solution.py:70
  117.5 5.4 %collective-permute-start.2 = (f32[2,2048]{1,0:T(2,128)S(1)}, f32[2,2048]{1,0:T(2,128)S(1)}, u32[]{:S(2)}, u32[]{:S(2)}) collective-permute-start(f32[2,2048]{1,0:T(2,128)S(1)} %fusion.30), channel_id=1, source_target_pairs={{0,16},{4,20},{8,24},{12,28},{16,0},{20,4},{24,8},{28,12},{1,17},{... | collective-permute-start | bytes 49160 | tf_op jit(solution)/shard_map/ppermute | solution.py:70
Sparse Core Ops, SparseCore 0:
  25.9 30.7 reduce-scatter.6
  99.6 129.8 reduce-scatter.4
